TPU v7x, 32 devices: a whole 2x2x4 slice. The times are simulated.
32 devices in a mesh: row: 8 (over z, x), col: 4 (over y, core).
Axes of the slice: x: 2, y: 2, z: 4, core: 2. Of those that a mesh axis runs over, the one named last changes fastest.
Arguments:
- offsets: int32 [8, 4, 2], P('row', 'col'), may hold values from 1 to 3
- targets: float32 [3, 3, 256, 512], P(None, None, 'row', 'col'), may hold values from -60 to 60
- grid_fine: float32 [32, 256, 512], P(None, 'row', 'col'), may hold values from -6 to 6
- grid_coarse: float32 [32, 64, 128], P(None, 'row', 'col'), may hold values from -6 to 6
- weight_in: float32 [512, 64], replicated, may hold values from -0.75 to 0.75
- weight_mid: float32 [1, 512, 512], replicated, may hold values from -0.25 to 0.25
- weight_out: float32 [3, 512], replicated, may hold values from -0.397747564 to 0.397747564
- fine_first: float32 [32, 256, 512], P(None, 'row', 'col'), may hold values from -0.012 to 0.012
- fine_second: float32 [32, 256, 512], P(None, 'row', 'col'), may hold values from 1e-06 to 0.0001
- coarse_first: float32 [32, 64, 128], P(None, 'row', 'col'), may hold values from -0.012 to 0.012
- coarse_second: float32 [32, 64, 128], P(None, 'row', 'col'), may hold values from 1e-06 to 0.0001
- in_first: float32 [512, 64], replicated, may hold values from -0.012 to 0.012
- in_second: float32 [512, 64], replicated, may hold values from 1e-06 to 0.0001
- mid_first: float32 [1, 512, 512], replicated, may hold values from -0.012 to 0.012
- mid_second: float32 [1, 512, 512], replicated, may hold values from 1e-06 to 0.0001
- out_first: float32 [3, 512], replicated, may hold values from -0.012 to 0.012
- out_second: float32 [3, 512], replicated, may hold values from 1e-06 to 0.0001
Outputs:
- fine_step: float32 [32, 256, 512], P(None, 'row', 'col')
- coarse_step: float32 [32, 64, 128], P(None, 'row', 'col')
- input_step: float32 [512, 64], replicated
- middle_step: float32 [1, 512, 512], replicated
- output_step: float32 [3, 512], replicated
All inputs are finite; a program needn't handle non-finite values.
Results may differ from a plain program's by a relative error of at most 0.0014.
The roundings to bfloat16 on the way count: a program that leaves them out, or rounds other values in their place, can miss the bound.
Values sent between devices are 32-bit elements; how exact they have to be, the bound alone decides.
A program may use at most 64 MiB of HBM per device.

v0:
```python
import jax
import jax.numpy as jnp
from jax import lax
from jax.sharding import PartitionSpec as P

SUB = 4
RATIO = 4
ADAM_STEP = 10
BETA_ONE = 0.9
BETA_TWO = 0.99
ADAM_EPSILON = 1e-08
CLIP_RMS = 0.01
LOSS_VALUE = 0.25
MEAN_EPSILON = 1e-06


def shifted(block, axis, distance):
    devices = range(lax.axis_size(axis))
    route = [(i - distance, i) for i in devices if i - distance in devices]
    return lax.ppermute(block, axis, route)


def interp_table(samples, level_ratio, offset):
    positions = jnp.arange(samples, dtype=jnp.int32)
    base_index = positions // level_ratio
    fraction = (
        (positions % level_ratio).astype(jnp.float32) + offset.astype(jnp.float32) / SUB
    ) / level_ratio
    column = jnp.arange(samples // level_ratio + 1, dtype=jnp.int32)
    lower_hit = (column[None, :] == base_index[:, None]).astype(jnp.float32)
    upper_hit = (column[None, :] == base_index[:, None] + 1).astype(jnp.float32)
    return lower_hit * (1.0 - fraction)[:, None] + upper_hit * fraction[:, None]


def level_tables(row_count, col_count, shift_y, shift_x):
    return (
        interp_table(row_count, 1, shift_y),
        interp_table(col_count, 1, shift_x),
        interp_table(row_count, RATIO, shift_y),
        interp_table(col_count, RATIO, shift_x),
    )


def sample_level(extended, row_table, col_table):
    across = jnp.einsum("kjl,ml->kjm", extended, col_table, precision=lax.Precision.HIGHEST)
    return jnp.einsum("ij,kjm->kim", row_table, across, precision=lax.Precision.HIGHEST)


def spread_level(cotangent, row_table, col_table):
    backward = jnp.einsum("ij,kim->kjm", row_table, cotangent, precision=lax.Precision.HIGHEST)
    return jnp.einsum("kjm,ml->kjl", backward, col_table, precision=lax.Precision.HIGHEST)


def sample_features(fine_ext, coarse_ext, tables):
    fine_feat = sample_level(fine_ext, tables[0], tables[1])
    coarse_feat = sample_level(coarse_ext, tables[2], tables[3])
    channels, row_count, col_count = fine_feat.shape
    return jnp.concatenate(
        [
            fine_feat.reshape(channels, row_count * col_count),
            coarse_feat.reshape(channels, row_count * col_count),
        ],
        axis=0,
    ).astype(jnp.bfloat16)


def spread_features(feature_grad, tables):
    channels = feature_grad.shape[0] // 2
    row_count = tables[0].shape[0]
    col_count = tables[1].shape[0]
    fine_cot = feature_grad[:channels].reshape(channels, row_count, col_count)
    coarse_cot = feature_grad[channels:].reshape(channels, row_count, col_count)
    return (
        spread_level(fine_cot, tables[0], tables[1]),
        spread_level(coarse_cot, tables[2], tables[3]),
    )


def matmul(former, latter):
    return jnp.dot(former, latter, preferred_element_type=jnp.float32)


def contract_rows(former, latter):
    return lax.dot_general(
        former, latter, (((0,), (0,)), ((), ())), preferred_element_type=jnp.float32
    )


def contract_cols(former, latter):
    return lax.dot_general(
        former, latter, (((1,), (1,)), ((), ())), preferred_element_type=jnp.float32
    )


def silu_slope(pre_act):
    sigmoid = jax.nn.sigmoid(pre_act)
    return sigmoid * (1.0 + pre_act * (1.0 - sigmoid))


def decoder_forward(features, low_in, low_mid, low_out):
    pre_acts = [matmul(low_in, features)]
    activations = [jax.nn.silu(pre_acts[0]).astype(jnp.bfloat16)]
    pre_acts.append(matmul(low_mid[0], activations[-1]))
    activations.append(jax.nn.silu(pre_acts[-1]).astype(jnp.bfloat16))
    return (matmul(low_out, activations[-1]), pre_acts, activations)


def decoder_backward(features, pre_acts, activations, cotangent, low_in, low_mid, low_out):
    out_cotangent = cotangent.astype(jnp.bfloat16)
    grad_out = contract_cols(out_cotangent, activations[-1])
    upward = contract_rows(low_out, out_cotangent)
    grads_mid = []
    delta_low = (upward * silu_slope(pre_acts[1])).astype(jnp.bfloat16)
    grads_mid.insert(0, contract_cols(delta_low, activations[0]))
    upward = contract_rows(low_mid[0], delta_low)
    delta_low = (upward * silu_slope(pre_acts[0])).astype(jnp.bfloat16)
    grad_in = contract_cols(delta_low, features)
    feature_grad = contract_rows(low_in, delta_low)
    return (grad_in, jnp.stack(grads_mid), grad_out, feature_grad)


def pixel_cotangent(value_error, row_error, row_prior, col_error, col_prior):
    return (
        2.0 * LOSS_VALUE * value_error
        + 2.0 * (row_prior - row_error)
        + 2.0 * (col_prior - col_error)
    )


def clip_factor(total, entries):
    return jnp.minimum(1.0, CLIP_RMS / jnp.sqrt(total / entries + MEAN_EPSILON))


def adam_step(gradient, moment_one, moment_two, clip_scale):
    clipped = gradient * clip_scale
    new_one = BETA_ONE * moment_one + (1.0 - BETA_ONE) * clipped
    new_two = BETA_TWO * moment_two + (1.0 - BETA_TWO) * clipped * clipped
    return (
        new_one
        / (1.0 - BETA_ONE**ADAM_STEP)
        / (jnp.sqrt(new_two / (1.0 - BETA_TWO**ADAM_STEP)) + ADAM_EPSILON)
    )


def grid_total_sum(grid_local):
    return lax.psum(grid_local, ("row", "col"))


def shards(
    offsets,
    targets,
    grid_fine,
    grid_coarse,
    weight_in,
    weight_mid,
    weight_out,
    fine_first,
    fine_second,
    coarse_first,
    coarse_second,
    in_first,
    in_second,
    mid_first,
    mid_second,
    out_first,
    out_second,
):
    channels, sample_rows, sample_cols = grid_fine.shape
    coarse_rows = grid_coarse.shape[1]
    coarse_cols = grid_coarse.shape[2]
    low_in = weight_in.astype(jnp.bfloat16)
    low_mid = weight_mid.astype(jnp.bfloat16)
    low_out = weight_out.astype(jnp.bfloat16)
    top_rows = jnp.concatenate([grid_fine[:, :1, :], grid_coarse[:, :1, :]], axis=2)
    top_rows = shifted(top_rows, "row", -1)
    fine_tall = jnp.concatenate([grid_fine, top_rows[:, :, :sample_cols]], axis=1)
    coarse_tall = jnp.concatenate([grid_coarse, top_rows[:, :, sample_cols:]], axis=1)
    edge_cols = jnp.concatenate([fine_tall[:, :, :1], coarse_tall[:, :, :1]], axis=1)
    edge_cols = shifted(edge_cols, "col", -1)
    fine_ext = jnp.concatenate([fine_tall, edge_cols[:, : sample_rows + 1, :]], axis=2)
    coarse_ext = jnp.concatenate([coarse_tall, edge_cols[:, sample_rows + 1 :, :]], axis=2)
    tables = level_tables(sample_rows, sample_cols, offsets[0, 0, 0], offsets[0, 0, 1])
    features = sample_features(fine_ext, coarse_ext, tables)
    predicted, pre_acts, activations = decoder_forward(features, low_in, low_mid, low_out)
    outputs = predicted.shape[0]
    predicted = predicted.reshape(outputs, sample_rows, sample_cols)
    below = shifted(predicted[:, :1, :], "row", -1)
    beside = shifted(predicted[:, :, :1], "col", -1)
    row_global = lax.axis_index("row") * sample_rows + jnp.arange(sample_rows, dtype=jnp.int32)
    col_global = lax.axis_index("col") * sample_cols + jnp.arange(sample_cols, dtype=jnp.int32)
    row_valid = (row_global < lax.axis_size("row") * sample_rows - 1)[None, :, None]
    col_valid = (col_global < lax.axis_size("col") * sample_cols - 1)[None, None, :]
    row_next = jnp.concatenate([predicted[:, 1:, :], below], axis=1)
    col_next = jnp.concatenate([predicted[:, :, 1:], beside], axis=2)
    value_error = predicted - targets[0]
    row_error = jnp.where(row_valid, row_next - predicted - targets[1], 0.0)
    col_error = jnp.where(col_valid, col_next - predicted - targets[2], 0.0)
    above = shifted(row_error[:, -1:, :], "row", 1)
    before = shifted(col_error[:, :, -1:], "col", 1)
    row_prior = jnp.concatenate([above, row_error[:, :-1, :]], axis=1)
    col_prior = jnp.concatenate([before, col_error[:, :, :-1]], axis=2)
    cotangent = pixel_cotangent(value_error, row_error, row_prior, col_error, col_prior)
    grad_in, grad_mid, grad_out, feature_grad = decoder_backward(
        features,
        pre_acts,
        activations,
        cotangent.reshape(outputs, sample_rows * sample_cols),
        low_in,
        low_mid,
        low_out,
    )
    fine_back, coarse_back = spread_features(feature_grad, tables)
    side_cols = jnp.concatenate(
        [fine_back[:, :, sample_cols:], coarse_back[:, :, coarse_cols:]], axis=1
    )
    side_cols = shifted(side_cols, "col", 1)
    fine_tall_grad = jnp.concatenate(
        [fine_back[:, :, :1] + side_cols[:, : sample_rows + 1, :], fine_back[:, :, 1:sample_cols]],
        axis=2,
    )
    coarse_tall_grad = jnp.concatenate(
        [
            coarse_back[:, :, :1] + side_cols[:, sample_rows + 1 :, :],
            coarse_back[:, :, 1:coarse_cols],
        ],
        axis=2,
    )
    bottom_rows = jnp.concatenate(
        [fine_tall_grad[:, sample_rows:, :], coarse_tall_grad[:, coarse_rows:, :]], axis=2
    )
    bottom_rows = shifted(bottom_rows, "row", 1)
    fine_grad = jnp.concatenate(
        [
            fine_tall_grad[:, :1, :] + bottom_rows[:, :, :sample_cols],
            fine_tall_grad[:, 1:sample_rows, :],
        ],
        axis=1,
    )
    coarse_grad = jnp.concatenate(
        [
            coarse_tall_grad[:, :1, :] + bottom_rows[:, :, sample_cols:],
            coarse_tall_grad[:, 1:coarse_rows, :],
        ],
        axis=1,
    )
    grid_local = jnp.sum(fine_grad * fine_grad) + jnp.sum(coarse_grad * coarse_grad)
    devices = lax.axis_size("row") * lax.axis_size("col")
    grid_entries = (fine_grad.size + coarse_grad.size) * devices
    decoder_entries = weight_in.size + weight_mid.size + weight_out.size
    grad_in, grad_mid, grad_out = lax.psum((grad_in, grad_mid, grad_out), ("row", "col"))
    grid_total = grid_total_sum(grid_local)
    decoder_total = (
        jnp.sum(grad_in * grad_in) + jnp.sum(grad_mid * grad_mid) + jnp.sum(grad_out * grad_out)
    )
    decoder_scale = clip_factor(decoder_total, decoder_entries)
    middle_step = adam_step(grad_mid, mid_first, mid_second, decoder_scale)
    grid_scale = clip_factor(grid_total, grid_entries)
    fine_step = adam_step(fine_grad, fine_first, fine_second, grid_scale)
    coarse_step = adam_step(coarse_grad, coarse_first, coarse_second, grid_scale)
    input_step = adam_step(grad_in, in_first, in_second, decoder_scale)
    output_step = adam_step(grad_out, out_first, out_second, decoder_scale)
    return (fine_step, coarse_step, input_step, middle_step, output_step)


def solution(mesh):
    placed = (
        P("row", "col", None),
        P(None, None, "row", "col"),
        P(None, "row", "col"),
        P(None, "row", "col"),
        P(),
        P(),
        P(),
        P(None, "row", "col"),
        P(None, "row", "col"),
        P(None, "row", "col"),
        P(None, "row", "col"),
        P(),
        P(),
        P(),
        P(),
        P(),
        P(),
    )
    return jax.shard_map(
        shards,
        mesh=mesh,
        in_specs=placed,
        out_specs=(P(None, "row", "col"), P(None, "row", "col"), P(), P(), P()),
        check_vma=False,
    )
```

profile of v0, /device:TPU:0, one launch (start us, length us, event | category | flops | bytes accessed | tf_op | source)
XLA Modules:
  0.0 238.9 jit_solution(828096831755790455)
XLA Ops:
  7.2 0.9 slice.117
  8.2 0.9 copy.59
  9.2 1.3 collective-permute-start
  10.5 1.3 fusion.148
  13.1 0.9 slice_bitcast_fusion.2
  14.0 1.9 collective-permute-done
  16.0 0.3 copy.64
  16.3 1.1 pad_maximum_fusion
  17.4 0.3 copy.63
  17.8 1.3 collective-permute-start.1
  19.1 1.8 collective-permute-done.1
  20.9 0.3 copy.66
  21.2 0.3 copy.65
  21.6 2.2 fusion.14
  23.8 0.6 convolution_convert_fusion.1
  24.6 0.3 fusion.37
  24.9 0.6 convolution_convert_fusion
  25.6 1.3 fusion.82
  26.9 4.4 %fusion.5 = (bf16[512,4096]{0,1:T(8,128)(2,1)S(1)}, f32[4096,512]{1,0:T(8,128)S(1)}) fusion(f32[1,512,512]{2,1,0:T(8,128)S(1)} %copy-done.11, f32[4096,512]{1,0:T(8,128)S(1)} %fusion.82), kind=kOutput, calls=%fused_computation.10 | convolution fusion | flops 2168717312 | bytes 22020096 | tf_op jit(solution)/shard_map/dot_general | solution.py:80
  31.4 1.2 fusion.125
  32.6 1.3 collective-permute-start.2
  33.9 1.3 collective-permute-start.4
  35.3 3.6 %collective-permute-done.4 = f32[3,32,1]{2,1,0:T(8,128)S(1)} collective-permute-done((f32[3,32,1]{2,1,0:T(8,128)S(1)}, f32[3,32,1]{2,1,0:T(8,128)S(1)}, u32[]{:S(2)}, u32[]{:S(2)}) %collective-permute-start.4) | collective-permute-done | bytes 416 | tf_op jit(solution)/shard_map/ppermute | solution.py:20
  39.1 4.6 %collective-permute-start.5 = (f32[3,32,1]{2,1,0:T(8,128)S(1)}, f32[3,32,1]{2,1,0:T(8,128)S(1)}, u32[]{:S(2)}, u32[]{:S(2)}) collective-permute-start(f32[3,32,1]{2,1,0:T(8,128)S(1)} %slice.167), channel_id=1, source_target_pairs={{0,1},{1,2},{2,3},{4,5},{5,6},{6,7},{8,9},{9,10},{10,11},{12,13},{... | collective-permute-start | bytes 1160 | tf_op jit(solution)/shard_map/ppermute | solution.py:20
  43.8 5.1 %collective-permute-start.3 = (f32[3,1,128]{2,1,0:T(1,128)S(1)}, f32[3,1,128]{2,1,0:T(1,128)S(1)}, u32[]{:S(2)}, u32[]{:S(2)}) collective-permute-start(f32[3,1,128]{2,1,0:T(1,128)S(1)} %slice.163), channel_id=1, source_target_pairs={{0,4},{4,8},{8,12},{12,16},{16,20},{20,24},{24,28},{1,5},{5,9},{9,... | collective-permute-start | bytes 4616 | tf_op jit(solution)/shard_map/ppermute | solution.py:20
  49.0 1.0 collective-permute-done.3
  50.1 0.2 fusion.63
  50.3 3.5 %fusion.1 = bf16[512,4096]{0,1:T(8,128)(2,1)S(1)} fusion(f32[4096,512]{1,0:T(8,128)S(1)} %get-tuple-element.27, bf16[3,4096]{1,0:T(4,128)(2,1)S(1)} %fusion.63, f32[3,512]{1,0:T(4,128)S(1)} %copy-done.8), kind=kOutput, calls=%fused_computation.3 | convolution fusion | flops 31458816 | bytes 12613632 | tf_op jit(solution)/shard_map/dot_general | solution.py:84
  53.8 3.4 %convolution_bitcast_fusion.1 = f32[1,512,512]{2,1,0:T(8,128)} fusion(bf16[512,4096]{0,1:T(8,128)(2,1)S(1)} %fusion.1, f32[4096,512]{1,0:T(8,128)S(1)} %fusion.82), kind=kOutput, calls=%fused_computation.24 | convolution fusion | flops 2157969408 | bytes 13631488 | tf_op jit(solution)/shard_map/dot_general | solution.py:90
  57.3 3.6 %fusion = bf16[512,4096]{0,1:T(8,128)(2,1)S(1)} fusion(f32[4096,512]{1,0:T(8,128)S(1)} %fusion.82, bf16[512,4096]{0,1:T(8,128)(2,1)S(1)} %fusion.1, f32[1,512,512]{2,1,0:T(8,128)S(1)} %copy-done.11), kind=kOutput, calls=%fused_computation.1 | convolution fusion | flops 2166620160 | bytes 17825792 | tf_op jit(solution)/shard_map/dot_general | solution.py:84
  60.9 2.0 copy-done.1
  62.8 1.4 convolution_bitcast_fusion
  64.3 0.1 copy.92
  64.4 0.4 convolution_bitcast_fusion.3
  64.8 0.3 fusion.43
  65.1 0.7 fusion.147
  65.8 0.3 copy.70
  66.2 0.8 convolution_bitcast_fusion.2
  67.0 1.2 fusion.56
  68.3 0.3 copy.69
  68.7 1.3 collective-permute-start.6
  70.0 3.7 %fusion.150 = f32[512,64]{0,1:T(8,128)} fusion(bf16[64,4096]{1,0:T(8,128)(2,1)S(1)} %bitcast_dynamic-update-slice_fusion, bf16[512,4096]{0,1:T(8,128)(2,1)} %copy-done.1), kind=kOutput, calls=%fused_computation.235 | convolution fusion | flops 268435456 | bytes 4849664 | tf_op jit(solution)/shard_map/dot_general | solution.py:90
  73.7 0.2 slice.175
  74.1 1.2 copy.74
  75.3 0.3 copy.71
  75.7 0.3 copy.76
  76.0 0.4 copy.72
  76.4 0.2 fusion.80
  76.6 4.9 %collective-permute-start.7 = (f32[32,1,160]{2,1,0:T(1,128)S(1)}, f32[32,1,160]{2,1,0:T(1,128)S(1)}, u32[]{:S(2)}, u32[]{:S(2)}) collective-permute-start(f32[32,1,160]{2,1,0:T(1,128)S(1)} %fusion.80), channel_id=1, source_target_pairs={{0,4},{4,8},{8,12},{12,16},{16,20},{20,24},{24,28},{1,5},{5,9},{9,... | collective-permute-start | bytes 61448 | tf_op jit(solution)/shard_map/ppermute | solution.py:20
  81.5 2.8 %fusion.149 = f32[3,512]{1,0:T(4,128)S(1)} fusion(bf16[3,4096]{1,0:T(4,128)(2,1)S(1)} %fusion.63, bf16[512,4096]{0,1:T(8,128)(2,1)} %copy-done), kind=kOutput, calls=%fused_computation.234 | convolution fusion | flops 12582912 | bytes 4225024 | tf_op jit(solution)/shard_map/dot_general | solution.py:90
  84.3 0.1 slice_add_fusion.1
  84.4 0.8 multiply_reduce_fusion.1
  85.2 0.1 slice_add_fusion
  85.3 0.7 multiply_reduce_fusion.3
  87.4 41.9 %all-reduce = (f32[]{:T(128)}, f32[3,512]{1,0:T(4,128)S(1)}) all-reduce(f32[]{:T(128)S(6)} %add.300, f32[3,512]{1,0:T(4,128)S(1)} %fusion.149), channel_id=1, replica_groups=mesh['row'=8,'col'=4] {'row','col'}, use_global_device_ids=true, to_apply=%region_2.3 | all-reduce | flops 1537 | bytes 12296 | tf_op jit(solution)/shard_map/psum | solution.py:146
  129.9 0.7 multiply_reduce_fusion.4
  130.6 1.7 fusion.49
  132.3 2.5 %fusion.29 = f32[32,32,128]{2,1,0:T(8,128)} fusion(f32[32,32,128]{2,1,0:T(8,128)} %param.25, f32[32,32,128]{2,1,0:T(8,128)} %param.24, f32[]{:T(128)S(6)} %min.6, f32[32,33,127]{2,1,0:T(8,128)S(1)} %slice.175, f32[32,33,1]{2,1,0:T(8,128)S(1)} %copy.72, f32[32,1,128]{2,1,0:T(1,128)S(1)} %slice_add_fusion.1), kind=kLoop, calls=%fused_computation.47 | loop fusion | flops 2228224 | bytes 2129924 | tf_op jit(solution)/shard_map/div | solution.py:139
  134.7 86.2 %all-reduce.4.cloned.1.call-done = (f32[512,64]{0,1:T(8,128)}, f32[1,512,512]{2,1,0:T(8,128)}) async-done(((f32[512,64]{0,1:T(8,128)}, f32[1,512,512]{2,1,0:T(8,128)}), (f32[512,64]{0,1:T(8,128)}, f32[1,512,512]{2,1,0:T(8,128)})) %all-reduce.4.cloned.1.call-update) | async-done | bytes 1179664 | tf_op jit(solution)/shard_map/psum | solution.py:250
  220.9 2.1 multiply_reduce_fusion
  223.0 1.5 multiply_reduce_fusion.2
  226.6 0.6 fusion.103
  227.2 3.2 %fusion.24 = f32[1,512,512]{2,1,0:T(8,128)} fusion(f32[1,512,512]{2,1,0:T(8,128)S(1)} %copy-done.2, f32[1,512,512]{2,1,0:T(8,128)} %get-tuple-element.8, f32[1,512,512]{2,1,0:T(8,128)} %param.30, f32[]{:T(128)S(6)} %min.7), kind=kLoop, calls=%fused_computation.39 | loop fusion | flops 3145728 | bytes 4194308 | tf_op jit(solution)/shard_map/div | solution.py:139
  230.4 1.7 fusion.54
  (65 shorter events, 1.7 us)
Async XLA Ops:
  7.2 18.5 %copy-start.3 = (f32[512,64]{0,1:T(8,128)S(1)}, f32[512,64]{0,1:T(8,128)}, u32[]{:S(2)}) copy-start(f32[512,64]{0,1:T(8,128)} %param.21) | copy-start | bytes 393220
  7.2 213.8 %all-reduce.4.cloned.1.call-start = ((), (), s32[]{:S(2)}) async-start(), calls=%async_computation | async-start | bytes 2359296 | tf_op jit(solution)/shard_map/psum | solution.py:250
  9.2 6.8 %collective-permute-start = (f32[32,1,160]{2,1,0:T(1,128)S(1)}, f32[32,1,160]{2,1,0:T(1,128)S(1)}, u32[]{:S(2)}, u32[]{:S(2)}) collective-permute-start(f32[32,1,160]{2,1,0:T(1,128)S(1)} %copy.60), channel_id=1, source_target_pairs={{4,0},{8,4},{12,8},{16,12},{20,16},{24,20},{28,24},{5,1},{9,5},{13... | collective-permute-start | bytes 61448 | tf_op jit(solution)/shard_map/ppermute | solution.py:20
  17.8 3.1 %collective-permute-start.1 = (f32[32,42,1]{1,0,2:T(8,128)S(1)}, f32[32,42,1]{1,0,2:T(8,128)S(1)}, u32[]{:S(2)}, u32[]{:S(2)}) collective-permute-start(f32[32,42,1]{1,0,2:T(8,128)S(1)} %pad_maximum_fusion.7), channel_id=1, source_target_pairs={{1,0},{2,1},{3,2},{5,4},{6,5},{7,6},{9,8},{10,9},{11,10},{13,12},{... | collective-permute-start | bytes 16136 | tf_op jit(solution)/shard_map/ppermute | solution.py:20
  23.8 3.1 %copy-start.11 = (f32[1,512,512]{2,1,0:T(8,128)S(1)}, f32[1,512,512]{2,1,0:T(8,128)}, u32[]{:S(2)}) copy-start(f32[1,512,512]{2,1,0:T(8,128)} %param.22) | copy-start | bytes 3145732
  26.9 4.4 %copy-start.8 = (f32[3,512]{1,0:T(4,128)S(1)}, f32[3,512]{1,0:T(4,128)}, u32[]{:S(2)}) copy-start(f32[3,512]{1,0:T(4,128)} %param.23) | copy-start | bytes 18436
  26.9 12.0 %copy-start.4 = (f32[3,3,32,128]{3,2,1,0:T(8,128)S(1)}, f32[3,3,32,128]{3,2,1,0:T(8,128)}, u32[]{:S(2)}) copy-start(f32[3,3,32,128]{3,2,1,0:T(8,128)} %param.18) | copy-start | bytes 442372
  31.4 22.5 %copy-start = (bf16[512,4096]{0,1:T(8,128)(2,1)}, bf16[512,4096]{0,1:T(8,128)(2,1)S(1)}, u32[]{:S(2)}) copy-start(bf16[512,4096]{0,1:T(8,128)(2,1)S(1)} %get-tuple-element.26) | copy-start | bytes 12582916
  32.6 6.4 %collective-permute-start.2 = (f32[3,1,128]{2,1,0:T(1,128)S(1)}, f32[3,1,128]{2,1,0:T(1,128)S(1)}, u32[]{:S(2)}, u32[]{:S(2)}) collective-permute-start(f32[3,1,128]{2,1,0:T(1,128)S(1)} %slice.162), channel_id=1, source_target_pairs={{4,0},{8,4},{12,8},{16,12},{20,16},{24,20},{28,24},{5,1},{9,5},{13... | collective-permute-start | bytes 4616 | tf_op jit(solution)/shard_map/ppermute | solution.py:20
  33.9 5.0 %collective-permute-start.4 = (f32[3,32,1]{2,1,0:T(8,128)S(1)}, f32[3,32,1]{2,1,0:T(8,128)S(1)}, u32[]{:S(2)}, u32[]{:S(2)}) collective-permute-start(f32[3,32,1]{2,1,0:T(8,128)S(1)} %bitcast.213), channel_id=1, source_target_pairs={{1,0},{2,1},{3,2},{5,4},{6,5},{7,6},{9,8},{10,9},{11,10},{13,12},{... | collective-permute-start | bytes 1160 | tf_op jit(solution)/shard_map/ppermute | solution.py:20
  39.1 9.8 %collective-permute-start.5 = (f32[3,32,1]{2,1,0:T(8,128)S(1)}, f32[3,32,1]{2,1,0:T(8,128)S(1)}, u32[]{:S(2)}, u32[]{:S(2)}) collective-permute-start(f32[3,32,1]{2,1,0:T(8,128)S(1)} %slice.167), channel_id=1, source_target_pairs={{0,1},{1,2},{2,3},{4,5},{5,6},{6,7},{8,9},{9,10},{10,11},{12,13},{... | collective-permute-start | bytes 1160 | tf_op jit(solution)/shard_map/ppermute | solution.py:20
  43.8 6.2 %collective-permute-start.3 = (f32[3,1,128]{2,1,0:T(1,128)S(1)}, f32[3,1,128]{2,1,0:T(1,128)S(1)}, u32[]{:S(2)}, u32[]{:S(2)}) collective-permute-start(f32[3,1,128]{2,1,0:T(1,128)S(1)} %slice.163), channel_id=1, source_target_pairs={{0,4},{4,8},{8,12},{12,16},{16,20},{20,24},{24,28},{1,5},{5,9},{9,... | collective-permute-start | bytes 4616 | tf_op jit(solution)/shard_map/ppermute | solution.py:20
  60.8 2.0 copy-start.1
  68.7 6.9 %collective-permute-start.6 = (f32[32,42,1]{1,0,2:T(8,128)S(1)}, f32[32,42,1]{1,0,2:T(8,128)S(1)}, u32[]{:S(2)}, u32[]{:S(2)}) collective-permute-start(f32[32,42,1]{1,0,2:T(8,128)S(1)} %pad_maximum_fusion.8), channel_id=1, source_target_pairs={{0,1},{1,2},{2,3},{4,5},{5,6},{6,7},{8,9},{9,10},{10,11},{12,13},{... | collective-permute-start | bytes 16136 | tf_op jit(solution)/shard_map/ppermute | solution.py:20
  73.6 57.0 %copy-start.5 = (f32[32,8,32]{2,1,0:T(8,128)S(1)}, f32[32,8,32]{2,1,0:T(8,128)}, u32[]{:S(2)}) copy-start(f32[32,8,32]{2,1,0:T(8,128)} %param.27) | copy-start | bytes 98308
  75.7 150.9 %copy-start.9 = (f32[3,512]{1,0:T(4,128)S(1)}, f32[3,512]{1,0:T(4,128)}, u32[]{:S(2)}) copy-start(f32[3,512]{1,0:T(4,128)} %param.33) | copy-start | bytes 18436
  75.7 150.9 %copy-start.10 = (f32[3,512]{1,0:T(4,128)S(1)}, f32[3,512]{1,0:T(4,128)}, u32[]{:S(2)}) copy-start(f32[3,512]{1,0:T(4,128)} %param.32) | copy-start | bytes 18436
  75.7 151.5 %copy-start.2 = (f32[1,512,512]{2,1,0:T(8,128)S(1)}, f32[1,512,512]{2,1,0:T(8,128)}, u32[]{:S(2)}) copy-start(f32[1,512,512]{2,1,0:T(8,128)} %param.31) | copy-start | bytes 3145732
  76.5 153.9 %copy-start.6 = (f32[512,64]{0,1:T(8,128)S(1)}, f32[512,64]{0,1:T(8,128)}, u32[]{:S(2)}) copy-start(f32[512,64]{0,1:T(8,128)} %param.29) | copy-start | bytes 393220
  76.5 153.8 %copy-start.7 = (f32[512,64]{0,1:T(8,128)S(1)}, f32[512,64]{0,1:T(8,128)}, u32[]{:S(2)}) copy-start(f32[512,64]{0,1:T(8,128)} %param.28) | copy-start | bytes 393220
  76.6 7.7 %collective-permute-start.7 = (f32[32,1,160]{2,1,0:T(1,128)S(1)}, f32[32,1,160]{2,1,0:T(1,128)S(1)}, u32[]{:S(2)}, u32[]{:S(2)}) collective-permute-start(f32[32,1,160]{2,1,0:T(1,128)S(1)} %fusion.80), channel_id=1, source_target_pairs={{0,4},{4,8},{8,12},{12,16},{16,20},{20,24},{24,28},{1,5},{5,9},{9,... | collective-permute-start | bytes 61448 | tf_op jit(solution)/shard_map/ppermute | solution.py:20
Sparse Core Ops, SparseCore 0:
  87.5 133.4 all-reduce.3
where the time goes:
time: 240 us; the launch traced here: 239 us
  waiting for transfers between devices  94.6 us (39%)
  blocking collectives  41.9 us (17%)
  matrix products  31.7 us (13%)
  starting transfers between devices  21.1 us (9%)
  between operations  19.8 us (8%)
  other arithmetic  17.7 us (7%)
  local copies, waits for them, and re-layouts  12.2 us (5%)
    psum x1, waiting for transfers between devices, shards(): lax.psum((grad_in, grad_mid, grad_out), ('row', 'col'))  86.2 us
    psum x1, blocking collectives, grid_total_sum(): return lax.psum(grid_local, ('row', 'col'))  41.9 us
    ppermute x8, starting transfers between devices, shifted(): return lax.ppermute(block, axis, route)  21.1 us
    dot_general x3, matrix products, contract_cols(): lax.dot_general(former, latter, (((1,), (1,)), ((), ())), preferred_eleme...  9.93 us
    div x5, other arithmetic, adam_step(): new_one / (1.0 - BETA_ONE ** ADAM_STEP)  9.62 us
    dot_general x3, matrix products, contract_rows(): lax.dot_general(former, latter, (((0,), (0,)), ((), ())), preferred_eleme...  8.45 us
    ppermute x8, waiting for transfers between devices, shifted(): return lax.ppermute(block, axis, route)  8.35 us
    dot_general x3, matrix products, matmul(): return jnp.dot(former, latter, preferred_element_type=jnp.float32)  6.85 us
  transfers between devices with their start and end apart: 9, of which 6 were waited for; matrix products, arithmetic and copies ran while one was open for 7% of the time, Pallas kernels for 0%

commit v1 on v0

--- a/solution.py
+++ b/solution.py
@@ -143,7 +143,7 @@
 
 
 def grid_total_sum(grid_local):
-    return lax.psum(grid_local, ("row", "col"))
+    return lax.psum(lax.psum(grid_local, "col"), "row")
 
 
 def shards(

time: 240 us -> 282 us (1.18)
  blocking collectives: 41.9 us -> 68.3 us
  waiting for transfers between devices: 94.6 us -> 108 us
    psum x1 -> x3, blocking collectives: 41.9 us -> 68.3 us  [the longest x1 40.3 us: shards(): lax.psum((grad_in, grad_mid, grad_out), ('row', 'col'))]
    psum x1, waiting for transfers between devices: 86.2 us -> 98.7 us  [shards(): lax.psum((grad_in, grad_mid, grad_out), ('row', 'col'))]
    unnamed x32 -> x28, local copies, waits for them, and re-layouts: 4.27 us -> 6.13 us
  transfers between devices with their start and end apart: 9 -> 9, of which waited for: 6 -> 6; matrix products, arithmetic and copies ran while one was open for 7% -> 5% of each run, Pallas kernels for 0% -> 0%
where the time goes in v1:
time: 282 us; the launch traced here: 281 us
  waiting for transfers between devices  108 us (38%)
  blocking collectives  68.3 us (24%)
  matrix products  31.7 us (11%)
  starting transfers between devices  21.5 us (8%)
  between operations  19.8 us (7%)
  other arithmetic  18.4 us (7%)
  local copies, waits for them, and re-layouts  12.5 us (4%)
    psum x1, waiting for transfers between devices, shards(): lax.psum((grad_in, grad_mid, grad_out), ('row', 'col'))  98.7 us
    psum x1, blocking collectives, shards(): lax.psum((grad_in, grad_mid, grad_out), ('row', 'col'))  40.3 us
    psum x2, blocking collectives, grid_total_sum(): return lax.psum(lax.psum(grid_local, 'col'), 'row')  28 us
    ppermute x8, starting transfers between devices, shifted(): return lax.ppermute(block, axis, route)  21.4 us
    dot_general x3, matrix products, contract_cols(): lax.dot_general(former, latter, (((1,), (1,)), ((), ())), preferred_eleme...  9.94 us
    div x5, other arithmetic, adam_step(): new_one / (1.0 - BETA_ONE ** ADAM_STEP)  9.7 us
    ppermute x8, waiting for transfers between devices, shifted(): return lax.ppermute(block, axis, route)  9.67 us
    dot_general x3, matrix products, contract_rows(): lax.dot_general(former, latter, (((0,), (0,)), ((), ())), preferred_eleme...  8.46 us
  transfers between devices with their start and end apart: 9, of which 6 were waited for; matrix products, arithmetic and copies ran while one was open for 5% of the time, Pallas kernels for 0%

profile of v1, /device:TPU:0, one launch (start us, length us, event | category | flops | bytes accessed | tf_op | source)
XLA Modules:
  0.0 280.6 jit_solution(12101694119807830584)
XLA Ops:
  7.2 1.0 copy.59
  8.2 0.9 slice.117
  9.2 1.3 collective-permute-start
  10.5 1.3 fusion.148
  13.1 0.9 slice_bitcast_fusion.2
  14.0 1.9 collective-permute-done
  16.0 0.3 copy.64
  16.3 1.1 pad_maximum_fusion
  17.4 0.3 copy.63
  17.8 1.3 collective-permute-start.1
  19.1 1.8 collective-permute-done.1
  20.9 0.3 copy.66
  21.2 0.3 copy.65
  21.6 2.2 fusion.14
  23.8 0.6 convolution_convert_fusion.1
  24.5 0.3 fusion.37
  24.9 0.6 convolution_convert_fusion
  25.6 1.3 fusion.82
  26.9 4.4 %fusion.5 = (bf16[512,4096]{0,1:T(8,128)(2,1)S(1)}, f32[4096,512]{1,0:T(8,128)S(1)}) fusion(f32[1,512,512]{2,1,0:T(8,128)S(1)} %copy-done.9, f32[4096,512]{1,0:T(8,128)S(1)} %fusion.82), kind=kOutput, calls=%fused_computation.10 | convolution fusion | flops 2168717312 | bytes 22020096 | tf_op jit(solution)/shard_map/dot_general | solution.py:80
  31.4 1.2 fusion.125
  32.6 1.3 collective-permute-start.4
  33.9 1.3 collective-permute-start.2
  35.3 2.3 collective-permute-done.4
  37.6 2.6 collective-permute-done.2
  40.4 3.5 %collective-permute-start.5 = (f32[3,32,1]{2,1,0:T(8,128)S(1)}, f32[3,32,1]{2,1,0:T(8,128)S(1)}, u32[]{:S(2)}, u32[]{:S(2)}) collective-permute-start(f32[3,32,1]{2,1,0:T(8,128)S(1)} %slice.167), channel_id=1, source_target_pairs={{0,1},{1,2},{2,3},{4,5},{5,6},{6,7},{8,9},{9,10},{10,11},{12,13},{... | collective-permute-start | bytes 1160 | tf_op jit(solution)/shard_map/ppermute | solution.py:20
  44.1 4.7 %collective-permute-start.3 = (f32[3,1,128]{2,1,0:T(1,128)S(1)}, f32[3,1,128]{2,1,0:T(1,128)S(1)}, u32[]{:S(2)}, u32[]{:S(2)}) collective-permute-start(f32[3,1,128]{2,1,0:T(1,128)S(1)} %slice.163), channel_id=1, source_target_pairs={{0,4},{4,8},{8,12},{12,16},{16,20},{20,24},{24,28},{1,5},{5,9},{9,... | collective-permute-start | bytes 4616 | tf_op jit(solution)/shard_map/ppermute | solution.py:20
  48.9 1.0 collective-permute-done.3
  49.9 0.2 fusion.63
  50.1 3.5 %fusion.1 = bf16[512,4096]{0,1:T(8,128)(2,1)S(1)} fusion(f32[4096,512]{1,0:T(8,128)S(1)} %get-tuple-element.25, bf16[3,4096]{1,0:T(4,128)(2,1)S(1)} %fusion.63, f32[3,512]{1,0:T(4,128)S(1)} %copy-done.6), kind=kOutput, calls=%fused_computation.3 | convolution fusion | flops 31458816 | bytes 12613632 | tf_op jit(solution)/shard_map/dot_general | solution.py:84
  53.7 3.4 %convolution_bitcast_fusion.1 = f32[1,512,512]{2,1,0:T(8,128)} fusion(bf16[512,4096]{0,1:T(8,128)(2,1)S(1)} %fusion.1, f32[4096,512]{1,0:T(8,128)S(1)} %fusion.82), kind=kOutput, calls=%fused_computation.24 | convolution fusion | flops 2157969408 | bytes 13631488 | tf_op jit(solution)/shard_map/dot_general | solution.py:90
  57.1 3.6 %fusion = bf16[512,4096]{0,1:T(8,128)(2,1)S(1)} fusion(f32[4096,512]{1,0:T(8,128)S(1)} %fusion.82, bf16[512,4096]{0,1:T(8,128)(2,1)S(1)} %fusion.1, f32[1,512,512]{2,1,0:T(8,128)S(1)} %copy-done.9), kind=kOutput, calls=%fused_computation.1 | convolution fusion | flops 2166620160 | bytes 17825792 | tf_op jit(solution)/shard_map/dot_general | solution.py:84
  60.7 2.0 copy-done.1
  62.7 1.4 convolution_bitcast_fusion
  64.0 0.9 slice_bitcast_fusion
  65.0 0.8 convolution_bitcast_fusion.2
  65.8 1.2 fusion.56
  67.1 0.3 copy.69
  67.4 1.1 copy.92
  68.6 0.4 convolution_bitcast_fusion.3
  69.0 0.3 fusion.43
  69.3 0.3 copy.70
  69.7 3.9 %collective-permute-start.6 = (f32[32,42,1]{1,0,2:T(8,128)S(1)}, f32[32,42,1]{1,0,2:T(8,128)S(1)}, u32[]{:S(2)}, u32[]{:S(2)}) collective-permute-start(f32[32,42,1]{1,0,2:T(8,128)S(1)} %pad_maximum_fusion.8), channel_id=1, source_target_pairs={{0,1},{1,2},{2,3},{4,5},{5,6},{6,7},{8,9},{9,10},{10,11},{12,13},{... | collective-permute-start | bytes 16136 | tf_op jit(solution)/shard_map/ppermute | solution.py:20
  73.7 3.7 %fusion.150 = f32[512,64]{0,1:T(8,128)} fusion(bf16[64,4096]{1,0:T(8,128)(2,1)S(1)} %bitcast_dynamic-update-slice_fusion, bf16[512,4096]{0,1:T(8,128)(2,1)} %copy-done.1), kind=kOutput, calls=%fused_computation.235 | convolution fusion | flops 268435456 | bytes 4849664 | tf_op jit(solution)/shard_map/dot_general | solution.py:90
  77.4 0.2 slice.175
  77.7 0.3 copy.74
  78.0 0.3 copy.71
  78.5 0.3 copy.76
  78.8 0.4 copy.72
  79.3 4.1 %collective-permute-start.7 = (f32[32,1,160]{2,1,0:T(1,128)S(1)}, f32[32,1,160]{2,1,0:T(1,128)S(1)}, u32[]{:S(2)}, u32[]{:S(2)}) collective-permute-start(f32[32,1,160]{2,1,0:T(1,128)S(1)} %fusion.80), channel_id=1, source_target_pairs={{0,4},{4,8},{8,12},{12,16},{16,20},{20,24},{24,28},{1,5},{5,9},{9,... | collective-permute-start | bytes 61448 | tf_op jit(solution)/shard_map/ppermute | solution.py:20
  83.5 2.8 %fusion.149 = f32[3,512]{1,0:T(4,128)S(1)} fusion(bf16[3,4096]{1,0:T(4,128)(2,1)S(1)} %fusion.63, bf16[512,4096]{0,1:T(8,128)(2,1)} %copy-done), kind=kOutput, calls=%fused_computation.234 | convolution fusion | flops 12582912 | bytes 4225024 | tf_op jit(solution)/shard_map/dot_general | solution.py:90
  86.3 40.3 %psum.39 = f32[3,512]{1,0:T(4,128)S(1)} all-reduce(f32[3,512]{1,0:T(4,128)S(1)} %fusion.149), channel_id=1, replica_groups=mesh['row'=8,'col'=4] {'row','col'}, use_global_device_ids=true, to_apply=%region_8.9 | all-reduce | flops 1536 | bytes 12288 | tf_op jit(solution)/shard_map/psum | solution.py:250
  126.7 1.4 multiply_reduce_fusion.3
  128.1 0.8 multiply_reduce_fusion.1
  130.3 6.5 %psum.35 = f32[]{:T(128)} all-reduce(f32[]{:T(128)S(6)} %add.302), channel_id=1, replica_groups=mesh['row'=8,'col'=4] {'col'}, use_global_device_ids=true, to_apply=%region_2.3 | all-reduce | flops 1 | bytes 8 | tf_op jit(solution)/shard_map/psum | solution.py:146
  136.8 0.7 multiply_reduce_fusion.4
  137.4 21.5 %psum.36 = f32[]{:T(128)} all-reduce(f32[]{:T(128)} %psum.35), channel_id=1, replica_groups=mesh['row'=8,'col'=4] {'row'}, use_global_device_ids=true, to_apply=%region_3.4 | all-reduce | flops 1 | bytes 8 | tf_op jit(solution)/shard_map/psum | solution.py:146
  159.6 1.8 fusion.49
  161.4 2.3 fusion.29
  163.7 98.7 %all-reduce.3.cloned.1.call-done = (f32[512,64]{0,1:T(8,128)}, f32[1,512,512]{2,1,0:T(8,128)}) async-done(((f32[512,64]{0,1:T(8,128)}, f32[1,512,512]{2,1,0:T(8,128)}), (f32[512,64]{0,1:T(8,128)}, f32[1,512,512]{2,1,0:T(8,128)})) %all-reduce.3.cloned.1.call-update) | async-done | bytes 1179664 | tf_op jit(solution)/shard_map/psum | solution.py:250
  262.4 2.1 multiply_reduce_fusion
  264.5 1.5 multiply_reduce_fusion.2
  268.1 0.6 fusion.103
  268.7 3.2 %fusion.24 = f32[1,512,512]{2,1,0:T(8,128)} fusion(f32[1,512,512]{2,1,0:T(8,128)S(1)} %copy-done.2, f32[1,512,512]{2,1,0:T(8,128)} %get-tuple-element.6, f32[1,512,512]{2,1,0:T(8,128)} %param.30, f32[]{:T(128)S(6)} %min.7), kind=kLoop, calls=%fused_computation.39 | loop fusion | flops 3145728 | bytes 4194308 | tf_op jit(solution)/shard_map/div | solution.py:139
  271.9 1.8 fusion.54
  (63 shorter events, 2.0 us)
Async XLA Ops:
  7.2 18.4 %copy-start.3 = (f32[512,64]{0,1:T(8,128)S(1)}, f32[512,64]{0,1:T(8,128)}, u32[]{:S(2)}) copy-start(f32[512,64]{0,1:T(8,128)} %param.21) | copy-start | bytes 393220
  7.2 255.3 %all-reduce.3.cloned.1.call-start = ((), (), s32[]{:S(2)}) async-start(), calls=%async_computation | async-start | bytes 2359296 | tf_op jit(solution)/shard_map/psum | solution.py:250
  9.2 6.8 %collective-permute-start = (f32[32,1,160]{2,1,0:T(1,128)S(1)}, f32[32,1,160]{2,1,0:T(1,128)S(1)}, u32[]{:S(2)}, u32[]{:S(2)}) collective-permute-start(f32[32,1,160]{2,1,0:T(1,128)S(1)} %copy.60), channel_id=1, source_target_pairs={{4,0},{8,4},{12,8},{16,12},{20,16},{24,20},{28,24},{5,1},{9,5},{13... | collective-permute-start | bytes 61448 | tf_op jit(solution)/shard_map/ppermute | solution.py:20
  17.8 3.1 %collective-permute-start.1 = (f32[32,42,1]{1,0,2:T(8,128)S(1)}, f32[32,42,1]{1,0,2:T(8,128)S(1)}, u32[]{:S(2)}, u32[]{:S(2)}) collective-permute-start(f32[32,42,1]{1,0,2:T(8,128)S(1)} %pad_maximum_fusion.7), channel_id=1, source_target_pairs={{1,0},{2,1},{3,2},{5,4},{6,5},{7,6},{9,8},{10,9},{11,10},{13,12},{... | collective-permute-start | bytes 16136 | tf_op jit(solution)/shard_map/ppermute | solution.py:20
  23.8 3.1 %copy-start.9 = (f32[1,512,512]{2,1,0:T(8,128)S(1)}, f32[1,512,512]{2,1,0:T(8,128)}, u32[]{:S(2)}) copy-start(f32[1,512,512]{2,1,0:T(8,128)} %param.22) | copy-start | bytes 3145732
  26.9 4.5 %copy-start.6 = (f32[3,512]{1,0:T(4,128)S(1)}, f32[3,512]{1,0:T(4,128)}, u32[]{:S(2)}) copy-start(f32[3,512]{1,0:T(4,128)} %param.23) | copy-start | bytes 18436
  26.9 13.3 %copy-start.5 = (f32[3,3,32,128]{3,2,1,0:T(8,128)S(1)}, f32[3,3,32,128]{3,2,1,0:T(8,128)}, u32[]{:S(2)}) copy-start(f32[3,3,32,128]{3,2,1,0:T(8,128)} %param.18) | copy-start | bytes 442372
  31.4 22.3 %copy-start = (bf16[512,4096]{0,1:T(8,128)(2,1)}, bf16[512,4096]{0,1:T(8,128)(2,1)S(1)}, u32[]{:S(2)}) copy-start(bf16[512,4096]{0,1:T(8,128)(2,1)S(1)} %get-tuple-element.24) | copy-start | bytes 12582916
  32.6 5.0 %collective-permute-start.4 = (f32[3,32,1]{2,1,0:T(8,128)S(1)}, f32[3,32,1]{2,1,0:T(8,128)S(1)}, u32[]{:S(2)}, u32[]{:S(2)}) collective-permute-start(f32[3,32,1]{2,1,0:T(8,128)S(1)} %bitcast.213), channel_id=1, source_target_pairs={{1,0},{2,1},{3,2},{5,4},{6,5},{7,6},{9,8},{10,9},{11,10},{13,12},{... | collective-permute-start | bytes 1160 | tf_op jit(solution)/shard_map/ppermute | solution.py:20
  33.9 6.4 %collective-permute-start.2 = (f32[3,1,128]{2,1,0:T(1,128)S(1)}, f32[3,1,128]{2,1,0:T(1,128)S(1)}, u32[]{:S(2)}, u32[]{:S(2)}) collective-permute-start(f32[3,1,128]{2,1,0:T(1,128)S(1)} %slice.162), channel_id=1, source_target_pairs={{4,0},{8,4},{12,8},{16,12},{20,16},{24,20},{28,24},{5,1},{9,5},{13... | collective-permute-start | bytes 4616 | tf_op jit(solution)/shard_map/ppermute | solution.py:20
  40.4 8.3 %collective-permute-start.5 = (f32[3,32,1]{2,1,0:T(8,128)S(1)}, f32[3,32,1]{2,1,0:T(8,128)S(1)}, u32[]{:S(2)}, u32[]{:S(2)}) collective-permute-start(f32[3,32,1]{2,1,0:T(8,128)S(1)} %slice.167), channel_id=1, source_target_pairs={{0,1},{1,2},{2,3},{4,5},{5,6},{6,7},{8,9},{9,10},{10,11},{12,13},{... | collective-permute-start | bytes 1160 | tf_op jit(solution)/shard_map/ppermute | solution.py:20
  44.1 5.8 %collective-permute-start.3 = (f32[3,1,128]{2,1,0:T(1,128)S(1)}, f32[3,1,128]{2,1,0:T(1,128)S(1)}, u32[]{:S(2)}, u32[]{:S(2)}) collective-permute-start(f32[3,1,128]{2,1,0:T(1,128)S(1)} %slice.163), channel_id=1, source_target_pairs={{0,4},{4,8},{8,12},{12,16},{16,20},{20,24},{24,28},{1,5},{5,9},{9,... | collective-permute-start | bytes 4616 | tf_op jit(solution)/shard_map/ppermute | solution.py:20
  60.7 2.0 copy-start.1
  69.7 8.7 %collective-permute-start.6 = (f32[32,42,1]{1,0,2:T(8,128)S(1)}, f32[32,42,1]{1,0,2:T(8,128)S(1)}, u32[]{:S(2)}, u32[]{:S(2)}) collective-permute-start(f32[32,42,1]{1,0,2:T(8,128)S(1)} %pad_maximum_fusion.8), channel_id=1, source_target_pairs={{0,1},{1,2},{2,3},{4,5},{5,6},{6,7},{8,9},{9,10},{10,11},{12,13},{... | collective-permute-start | bytes 16136 | tf_op jit(solution)/shard_map/ppermute | solution.py:20
  77.3 84.1 %copy-start.4 = (f32[32,32,128]{2,1,0:T(8,128)S(1)}, f32[32,32,128]{2,1,0:T(8,128)}, u32[]{:S(2)}) copy-start(f32[32,32,128]{2,1,0:T(8,128)} %param.25) | copy-start | bytes 1572868
  78.5 189.6 %copy-start.7 = (f32[3,512]{1,0:T(4,128)S(1)}, f32[3,512]{1,0:T(4,128)}, u32[]{:S(2)}) copy-start(f32[3,512]{1,0:T(4,128)} %param.33) | copy-start | bytes 18436
  78.5 189.6 %copy-start.8 = (f32[3,512]{1,0:T(4,128)S(1)}, f32[3,512]{1,0:T(4,128)}, u32[]{:S(2)}) copy-start(f32[3,512]{1,0:T(4,128)} %param.32) | copy-start | bytes 18436
  78.5 190.2 %copy-start.2 = (f32[1,512,512]{2,1,0:T(8,128)S(1)}, f32[1,512,512]{2,1,0:T(8,128)}, u32[]{:S(2)}) copy-start(f32[1,512,512]{2,1,0:T(8,128)} %param.31) | copy-start | bytes 3145732
  79.3 47.2 %collective-permute-start.7 = (f32[32,1,160]{2,1,0:T(1,128)S(1)}, f32[32,1,160]{2,1,0:T(1,128)S(1)}, u32[]{:S(2)}, u32[]{:S(2)}) collective-permute-start(f32[32,1,160]{2,1,0:T(1,128)S(1)} %fusion.80), channel_id=1, source_target_pairs={{0,4},{4,8},{8,12},{12,16},{16,20},{20,24},{24,28},{1,5},{5,9},{9,... | collective-permute-start | bytes 61448 | tf_op jit(solution)/shard_map/ppermute | solution.py:20
Sparse Core Ops, SparseCore 0:
  130.4 131.9 all-reduce.2
